TPU v7x, 32 devices: a whole 2x2x4 slice. The times are simulated.
32 devices in a mesh: tm: 16 (over z, y, x), rep: 2 (over core).
Axes of the slice: x: 2, y: 2, z: 4, core: 2. Of those that a mesh axis runs over, the one named last changes fastest.
Arguments:
- rows: float32 [65536, 256], P('tm', 'rep'), may hold values from -90 to 90, as said below
- row_mask: int32 [65536], P('tm'), may hold values from 0 to 1, as said below
- key_bucket: int32 [65536], P('tm'), may hold values from 0 to 15
- gain: float32 [256], P('rep'), may hold values from 0.1 to 1.9
Outputs:
- keyed: float32 [49152, 256], P('tm', 'rep')
Inputs may be any that keep to these rules, and one draw needn't show every extreme that they name: `rows`: scale per column differs; entries stay in the range. `row_mask`: of the 4096 rows of each index of tm, at least 2048 pass. Among the passing rows of one index of tm, no key bucket occurs more than 192 times, and one bucket, the same for all indices, occurs exactly 192 times on every index.
All inputs are finite; a program needn't handle non-finite values.
Results may differ from a plain program's by a relative error of at most 0.0003.
Values sent between devices are 32-bit elements; how exact they have to be, the bound alone decides.
A program may use at most 64 MiB of HBM per device.

v0:
```python
import jax
import jax.numpy as jnp
from jax import lax
from jax.sharding import PartitionSpec as P

F = 256
WINDOW = 512
epsilon = 1e-06


def passed_along(x, axis, by):
    devices = lax.axis_size(axis)
    return lax.ppermute(x, axis, [(i, (i + by) % devices) for i in range(devices)])


def window_sums(extended, width):
    blocks = extended.reshape(-1, width, extended.shape[1])
    steps = jnp.arange(width, dtype=jnp.int32)
    lower = (steps[:, None] >= steps[None, :]).astype(jnp.float32)
    inner = jnp.einsum("ij,bjf->bif", lower, blocks, precision=lax.Precision.HIGHEST)
    totals = inner[:, -1:, :]
    result = inner[1:] + totals[:-1] - inner[:-1]
    return result.reshape(-1, extended.shape[1])


def bucket_ranks(hits):
    size_rows, buckets = hits.shape
    block = min(512, size_rows)
    grouped = hits.reshape(size_rows // block, block, buckets)
    steps = jnp.arange(block, dtype=jnp.int32)
    lower = (steps[:, None] >= steps[None, :]).astype(jnp.float32)
    within = jnp.einsum("ij,bjc->bic", lower, grouped, precision=lax.Precision.HIGHEST)
    totals = within[:, -1, :]
    earlier = jnp.cumsum(totals, axis=0) - totals
    running = (within + earlier[:, None, :]).reshape(size_rows, buckets)
    local_rank = (jnp.sum(running * hits, axis=1) - 1.0).astype(jnp.int32)
    counts = jnp.sum(totals, axis=0).astype(jnp.int32)
    return (local_rank, counts)


def compact_rows(payload, row_mask):
    size_rows, width = payload.shape
    live = row_mask == 1
    order_rank = jnp.cumsum(row_mask) - 1
    target = jnp.where(live, order_rank, size_rows)
    return jnp.zeros((size_rows, width), jnp.float32).at[target].set(payload, mode="drop")


def fill_slots(values, slot, slots_total):
    width = values.shape[1]
    return jnp.zeros((slots_total, width), jnp.float32).at[slot].set(values, mode="drop")


def local(rows, row_mask, key_bucket, gain):
    size_rows, half = rows.shape
    nodes = lax.axis_size("tm")
    most = 3 * size_rows // (4 * nodes)
    positions = jnp.arange(size_rows, dtype=jnp.int32)
    bucket_ids = jnp.arange(nodes, dtype=jnp.int32)
    count = jnp.sum(row_mask)
    own_hits = (key_bucket[:, None] == bucket_ids[None, :]).astype(jnp.float32)
    payload = jnp.concatenate([rows, own_hits], axis=1)
    packed = compact_rows(payload, row_mask)
    compact = packed[:, :half]
    hits = packed[:, half:]
    valid = positions < count
    key_value = jnp.dot(
        hits,
        bucket_ids.astype(jnp.float32),
        precision=lax.Precision.HIGHEST,
        preferred_element_type=jnp.float32,
    )
    compact_key = jnp.where(valid, key_value.astype(jnp.int32), nodes)
    tail = lax.dynamic_slice_in_dim(compact, count - WINDOW, WINDOW, 0)
    earlier_tail = passed_along(tail, "tm", 1)
    extended = jnp.concatenate([earlier_tail, compact], axis=0)
    sums = window_sums(extended, WINDOW)
    squares = jnp.sum(sums * sums, axis=1)
    full = lax.psum(squares, "rep")
    values = sums * gain[None, :] / jnp.sqrt(full[:, None] / F + epsilon)
    local_rank, counts = bucket_ranks(hits)
    slot = jnp.where(valid, compact_key * most + local_rank, nodes * most)
    outgoing = fill_slots(values, slot, nodes * most)
    outgoing = outgoing.reshape(nodes, most * half)
    sideband = counts.astype(jnp.float32)[:, None]
    received, got_side = (
        lax.all_to_all(outgoing, "tm", split_axis=0, concat_axis=0, tiled=True),
        lax.all_to_all(sideband, "tm", split_axis=0, concat_axis=0, tiled=True),
    )
    got_numbers = got_side.astype(jnp.int32)
    got_starts = jnp.cumsum(got_numbers, axis=0) - got_numbers
    capacity = nodes * most
    start_list = got_starts.reshape(-1)
    spots = jnp.arange(capacity, dtype=jnp.int32)
    sender = jnp.sum((start_list[None, :] <= spots[:, None]).astype(jnp.int32), axis=1) - 1
    sender = jnp.maximum(sender, 0)
    offset = spots - start_list[sender]
    inside = (offset >= 0) & (offset < most)
    lookup = sender * most + jnp.clip(offset, 0, most - 1)
    flat = received.reshape(-1, half)
    keyed = jnp.where(inside[:, None], flat[lookup], jnp.float32(0.0))
    return keyed


def solution(mesh):
    in_specs = (P("tm", "rep"), P("tm"), P("tm"), P("rep"))
    out_specs = P("tm", "rep")
    return jax.shard_map(local, mesh=mesh, in_specs=in_specs, out_specs=out_specs, check_vma=False)
```

profile of v0, /device:TPU:12, one launch (start us, length us, event | category | flops | bytes accessed | tf_op | source)
XLA Modules:
  0.0 128.5 jit_solution(7532041285759532426)
XLA Ops:
  0.0 1.0 reduce-window.14
  1.0 0.1 slice.54
  1.1 0.1 reduce-window.18
  1.1 0.1 slice_reduce_fusion.2
  1.2 1.4 %fusion.20 = (s32[]{:T(128)}, s32[4096]{0:T(1024)S(1)}) fusion(s32[4096]{0:T(1024)} %param.5, s32[32,128]{1,0:T(8,128)S(1)} %reduce-window.14, s32[32]{0:T(128)S(1)} %slice_reduce_fusion.2), kind=kLoop, calls=%fused_computation.53 | loop fusion | flops 32767 | bytes 49284 | tf_op jit(solution)/shard_map/reduce_sum | solution.py:60
  2.7 1.3 %fusion.7 = f32[4096,16]{1,0:T(8,128)S(1)} fusion(s32[4096]{0:T(1024)} %param.6), kind=kLoop, calls=%fused_computation.17 | loop fusion | flops 131072 | bytes 278528 | tf_op jit(solution)/shard_map/convert_element_type | solution.py:61
  4.0 20.2 %scatter_custom_fusion = f32[4096,144]{1,0:T(8,128)} fusion(s32[4096]{0:T(1024)S(1)} %get-tuple-element.10, f32[4096,16]{1,0:T(8,128)S(1)} %fusion.7, f32[]{:T(128)} %constant.74, f32[4096,128]{1,0:T(8,128)} %param.4, f32[]{:T(128)} %constant.14.clone.1), kind=kCustom, calls=%fused_computation.3 | custom fusion | flops 589824 | bytes 6553608 | tf_op jit(solution)/shard_map/scatter | solution.py:46
  24.2 1.7 %slice.58 = f32[4096,128]{1,0:T(8,128)S(1)} slice(f32[4096,144]{1,0:T(8,128)} %scatter_custom_fusion), slice={[0:4096], [0:128]} | slice | bytes 4194304 | tf_op jit(solution)/shard_map/slice | solution.py:64
  25.9 0.0 copy-start
  27.3 0.0 copy-done
  27.3 0.0 slice-start
  27.3 1.5 %collective-permute-start = (f32[512,128]{1,0:T(8,128)S(1)}, f32[512,128]{1,0:T(8,128)S(1)}, u32[]{:S(2)}, u32[]{:S(2)}) collective-permute-start(f32[512,128]{1,0:T(8,128)S(1)} %constant_dynamic-slice_fusion), channel_id=1, source_target_pairs={{0,2},{2,4},{4,6},{6,8},{8,10},{10,12},{12,14},{14,16},{16,18},{18... | collective-permute-start | bytes 786440 | tf_op jit(solution)/shard_map/ppermute | solution.py:13
  28.9 0.0 slice-done
  28.9 3.4 %convolution_bitcast_fusion.1 = f32[8,512,16]{1,2,0:T(8,128)S(1)} fusion(f32[8,512,16]{2,1,0:T(8,128)S(1)} %bitcast.56), kind=kOutput, calls=%fused_computation.19 | convolution fusion | flops 402915328 | bytes 524288 | tf_op jit(solution)/shard_map/ij,bjc->bic/dot_general | solution.py:32
  32.3 0.2 slice_reduce_fusion.1
  32.5 0.7 copy.33
  33.2 7.2 %all-to-all-start = ((f32[16,1,1]{2,1,0:T(1,128)}), f32[16,1,1]{2,1,0:T(1,128)S(1)}, u32[]{:S(2)}, u32[]{:S(2)}) async-start(f32[16,1,1]{2,1,0:T(1,128)} %copy.33), calls=%async_computation | async-start | bytes 16384 | tf_op jit(solution)/shard_map/all_to_all | solution.py:88
  40.4 0.2 fusion.22
  40.5 3.5 %fusion.15 = f32[1,4096]{1,0:T(1,128)S(1)} fusion(f32[4096,144]{1,0:T(8,128)} %scatter_custom_fusion), kind=kOutput, calls=%fused_computation.45 | convolution fusion | flops 786448 | bytes 2113536 | tf_op jit(solution)/shard_map/dot_general | solution.py:67
  44.0 0.1 broadcast_add_fusion
  44.1 0.6 copy.43
  44.8 0.0 copy-start.1
  44.8 2.6 %fusion.5 = f32[4096]{0:T(1024)S(1)} fusion(f32[8,512,16]{2,1,0:T(8,128)S(1)} %copy.43, f32[4096,144]{1,0:T(8,128)} %scatter_custom_fusion), kind=kLoop, calls=%fused_computation.13 | loop fusion | flops 126976 | bytes 540672 | tf_op jit(solution)/shard_map/reduce_sum | solution.py:36
  47.3 0.7 compare_select_fusion.1
  48.0 0.0 collective-permute-done
  48.0 0.0 copy-done.1
  48.0 0.2 pad_maximum_fusion
  48.2 3.9 %convolution_bitcast_fusion = f32[9,512,128]{1,2,0:T(8,128)S(1)} fusion(f32[9,512,128]{2,1,0:T(8,128)S(1)} %bitcast.57), kind=kOutput, calls=%fused_computation.18 | convolution fusion | flops 3624140800 | bytes 4718592 | tf_op jit(solution)/shard_map/ij,bjf->bif/dot_general | solution.py:20
  52.1 0.4 slice_reduce_fusion
  52.5 1.8 %multiply_reduce_fusion = (f32[8,512]{1,0:T(8,128)S(1)}, f32[8,512,128]{1,2,0:T(8,128)}) fusion(f32[9,512,128]{1,2,0:T(8,128)S(1)} %convolution_bitcast_fusion, f32[8,128]{1,0:T(8,128)S(1)} %slice_reduce_fusion), kind=kLoop, calls=%fused_computation.14 | loop fusion | flops 2093056 | bytes 6311936 | tf_op jit(solution)/shard_map/reduce_sum | solution.py:78
  54.2 0.0 copy-start.2
  54.2 1.9 %copy.38 = f32[8,512,128]{2,1,0:T(8,128)S(1)} copy(f32[8,512,128]{1,2,0:T(8,128)} %get-tuple-element.8) | data formatting | bytes 4194304 | tf_op jit(solution)/shard_map/sub | solution.py:22
  56.2 3.4 %psum.7 = f32[4096]{0:T(1024)S(1)} all-reduce(f32[4096]{0:T(1024)S(1)} %bitcast.61), channel_id=1, replica_groups=mesh['tm'=16,'rep'=2] {'rep'}, use_global_device_ids=true, to_apply=%region_10.11 | all-reduce | flops 4096 | bytes 32768 | tf_op jit(solution)/shard_map/psum | solution.py:79
  59.6 0.0 copy-done.2
  59.6 1.9 %fusion.4 = f32[4096,128]{1,0:T(8,128)} fusion(f32[8,512,128]{2,1,0:T(8,128)S(1)} %copy.38, f32[4096]{0:T(1024)S(1)} %add_sqrt_fusion, f32[128]{0:T(128)S(1)} %copy-done.2), kind=kLoop, calls=%fused_computation.11 | loop fusion | flops 1048576 | bytes 4211200 | tf_op jit(solution)/shard_map/div | solution.py:80
  61.5 12.1 %scatter_custom_fusion.1 = f32[3072,128]{1,0:T(8,128)} fusion(s32[4096]{0:T(1024)S(1)} %compare_select_fusion.1, f32[4096,128]{1,0:T(8,128)} %fusion.4, f32[]{:T(128)} %constant.14.clone.1), kind=kCustom, calls=%fused_computation.24 | custom fusion | bytes 1573376 | tf_op jit(solution)/shard_map/scatter | solution.py:51
  73.6 0.0 all-to-all-done
  73.6 6.9 %all-to-all-start.1 = ((f32[16,1,24576]{2,1,0:T(1,128)}), f32[16,1,24576]{2,1,0:T(1,128)S(1)}, u32[]{:S(2)}, u32[]{:S(2)}) async-start(f32[16,1,24576]{2,1,0:T(1,128)} %bitcast.29), calls=%async_computation.1 | async-start | bytes 3145728 | tf_op jit(solution)/shard_map/all_to_all | solution.py:87
  80.6 0.1 reduce.3
  80.7 0.4 convert_reduce_fusion.1
  81.1 0.7 fusion.21
  81.8 0.1 convert_reduce_fusion
  81.9 9.9 %compare_and_fusion = (pred[3072]{0:T(1024)(128)(4,1)S(1)}, s32[3072]{0:T(1024)S(1)}) fusion(s32[]{:T(128)} %bitcast.22, s32[]{:T(128)} %bitcast.21, s32[]{:T(128)} %bitcast.20, s32[]{:T(128)} %bitcast.19, s32[]{:T(128)} %bitcast.18, s32[]{:T(128)} %bitcast.17, s32[]{:T(128)} %bitcast.16, s32[]{:T(128)} %bitcast.15, s32[]{:T(128)} %bitcast.14, s32[]{:T(128)} %bitcast.13, ...), kind=kLoop, calls=%fused_computation.42 | loop fusion | flops 110592 | bytes 27712 | tf_op jit(solution)/shard_map/and | solution.py:98
  91.9 26.0 %all-to-all-done.1 = f32[16,1,24576]{2,1,0:T(1,128)S(1)} async-done(((f32[16,1,24576]{2,1,0:T(1,128)}), f32[16,1,24576]{2,1,0:T(1,128)S(1)}, u32[]{:S(2)}, u32[]{:S(2)}) %all-to-all-start.1) | async-done | bytes 1572896 | tf_op jit(solution)/shard_map/all_to_all | solution.py:87
  117.9 8.1 %gather_fusion = f32[3072,128]{1,0:T(8,128)S(1)} fusion(f32[3072,128]{1,0:T(8,128)S(1)} %bitcast.55, s32[3072]{0:T(1024)S(1)} %broadcast_clamp_fusion), kind=kCustom, calls=%fused_computation | custom fusion | bytes 3158016 | tf_op jit(solution)/shard_map/gather | solution.py:101
  126.0 2.5 %broadcast_select_fusion = f32[3072,128]{1,0:T(8,128)} fusion(f32[3072,128]{1,0:T(8,128)S(1)} %gather_fusion, pred[3072]{0:T(1024)(128)(4,1)S(1)} %get-tuple-element.5), kind=kLoop, calls=%fused_computation.23 | loop fusion | flops 393216 | bytes 3148800 | tf_op jit(solution)/shard_map/jit(_where)/select_n | solution.py:101
  (10 shorter events, 0.2 us)
Async XLA Ops:
  25.9 1.4 %copy-start = (f32[4096,128]{1,0:T(8,128)}, f32[4096,128]{1,0:T(8,128)S(1)}, u32[]{:S(2)}) copy-start(f32[4096,128]{1,0:T(8,128)S(1)} %slice.58) | copy-start | bytes 6291460
  27.3 1.6 %slice-start = ((f32[4096,144]{1,0:T(8,128)}), f32[4096,16]{1,0:T(8,128)S(1)}, s32[]{:S(2)}) async-start(f32[4096,144]{1,0:T(8,128)} %scatter_custom_fusion), calls=%async_computation.2 | async-start | bytes 4194304 | tf_op jit(solution)/shard_map/slice | solution.py:65
  27.3 20.7 %collective-permute-start = (f32[512,128]{1,0:T(8,128)S(1)}, f32[512,128]{1,0:T(8,128)S(1)}, u32[]{:S(2)}, u32[]{:S(2)}) collective-permute-start(f32[512,128]{1,0:T(8,128)S(1)} %constant_dynamic-slice_fusion), channel_id=1, source_target_pairs={{0,2},{2,4},{4,6},{6,8},{8,10},{10,12},{12,14},{14,16},{16,18},{18... | collective-permute-start | bytes 786440 | tf_op jit(solution)/shard_map/ppermute | solution.py:13
  33.2 40.4 %all-to-all-start = ((f32[16,1,1]{2,1,0:T(1,128)}), f32[16,1,1]{2,1,0:T(1,128)S(1)}, u32[]{:S(2)}, u32[]{:S(2)}) async-start(f32[16,1,1]{2,1,0:T(1,128)} %copy.33), calls=%async_computation | async-start | bytes 16384 | tf_op jit(solution)/shard_map/all_to_all | solution.py:88
  44.8 3.3 %copy-start.1 = (f32[4096,128]{1,0:T(8,128)S(1)}, f32[4096,128]{1,0:T(8,128)}, u32[]{:S(2)}) copy-start(f32[4096,128]{1,0:T(8,128)} %copy-done) | copy-start | bytes 6291460
  54.2 5.3 %copy-start.2 = (f32[128]{0:T(128)S(1)}, f32[128]{0:T(128)}, u32[]{:S(2)}) copy-start(f32[128]{0:T(128)} %param.7) | copy-start | bytes 1540
  73.6 44.3 %all-to-all-start.1 = ((f32[16,1,24576]{2,1,0:T(1,128)}), f32[16,1,24576]{2,1,0:T(1,128)S(1)}, u32[]{:S(2)}, u32[]{:S(2)}) async-start(f32[16,1,24576]{2,1,0:T(1,128)} %bitcast.29), calls=%async_computation.1 | async-start | bytes 3145728 | tf_op jit(solution)/shard_map/all_to_all | solution.py:87
where the time goes:
time: 129 us
  other arithmetic  44.6 us (35%)
  local copies, waits for them, and re-layouts  26.5 us (21%)
  waiting for transfers between devices  26 us (20%)
  starting transfers between devices  15.6 us (12%)
  matrix products  10.8 us (8%)
  blocking collectives  3.36 us (3%)
  between operations  1.56 us (1%)
    all_to_all x1, waiting for transfers between devices, local(): lax.all_to_all(outgoing, 'tm', split_axis=0, concat_axis=0, tiled=True)  26 us
    scatter x1, other arithmetic, compact_rows(): jnp.zeros((size_rows, width), jnp.float32).at[target]  20.2 us
    scatter x1, local copies, waits for them, and re-layouts, fill_slots(): jnp.zeros((slots_total, width), jnp.float32).at[slot]  12.1 us
    and x1, other arithmetic, local(): inside = (offset >= 0) & (offset < most)  9.94 us
    gather x1, local copies, waits for them, and re-layouts, local(): keyed = jnp.where(inside[:, None], flat[lookup], jnp.float32(0.0))  8.11 us
    all_to_all x1, starting transfers between devices, local(): lax.all_to_all(sideband, 'tm', split_axis=0, concat_axis=0, tiled=True)  7.17 us
    all_to_all x1, starting transfers between devices, local(): lax.all_to_all(outgoing, 'tm', split_axis=0, concat_axis=0, tiled=True)  6.92 us
    dot_general x1, matrix products, window_sums(): jnp.einsum('ij,bjf->bif', lower, blocks, precision=lax.Precision.HIGHEST)  3.91 us
  transfers between devices with their start and end apart: 3, of which 1 were waited for; matrix products, arithmetic and copies ran while one was open for 35% of the time, Pallas kernels for 0%

commit v1 on v0

--- a/solution.py
+++ b/solution.py
@@ -2,6 +2,7 @@
 import jax.numpy as jnp
 from jax import lax
 from jax.sharding import PartitionSpec as P
+from jax.lax import all_gather
 
 F = 256
 WINDOW = 512
@@ -76,7 +77,11 @@
     extended = jnp.concatenate([earlier_tail, compact], axis=0)
     sums = window_sums(extended, WINDOW)
     squares = jnp.sum(sums * sums, axis=1)
-    full = lax.psum(squares, "rep")
+
+    def post_counts_in(matrix):
+        return all_gather(matrix, axis_name="rep").sum(axis=0)
+
+    full = post_counts_in(squares)
     values = sums * gain[None, :] / jnp.sqrt(full[:, None] / F + epsilon)
     local_rank, counts = bucket_ranks(hits)
     slot = jnp.where(valid, compact_key * most + local_rank, nodes * most)

time: 129 us -> 128 us (level)
  blocking collectives: 3.36 us -> 1.83 us
    psum x1 -> x0, blocking collectives: 3.36 us -> none  [local(): full = lax.psum(squares, 'rep')]
    all_gather x0 -> x1, blocking collectives: none -> 1.83 us  [post_counts_in(): return all_gather(matrix, axis_name='rep').sum(axis=0)]
  transfers between devices with their start and end apart: 3 -> 3, of which waited for: 1 -> 1; matrix products, arithmetic and copies ran while one was open for 35% -> 36% of each run, Pallas kernels for 0% -> 0%
where the time goes in v1:
time: 128 us; the launch traced here: 127 us
  other arithmetic  44.7 us (35%)
  local copies, waits for them, and re-layouts  26.5 us (21%)
  waiting for transfers between devices  25.9 us (20%)
  starting transfers between devices  15.6 us (12%)
  matrix products  10.8 us (8%)
  blocking collectives  1.83 us (1%)
  between operations  1.57 us (1%)
    all_to_all x1, waiting for transfers between devices, local(): lax.all_to_all(outgoing, 'tm', split_axis=0, concat_axis=0, tiled=True)  25.9 us
    scatter x1, other arithmetic, compact_rows(): jnp.zeros((size_rows, width), jnp.float32).at[target]  20.2 us
    scatter x1, local copies, waits for them, and re-layouts, fill_slots(): jnp.zeros((slots_total, width), jnp.float32).at[slot]  12.1 us
    and x1, other arithmetic, local(): inside = (offset >= 0) & (offset < most)  9.94 us
    gather x1, local copies, waits for them, and re-layouts, local(): keyed = jnp.where(inside[:, None], flat[lookup], jnp.float32(0.0))  8.11 us
    all_to_all x1, starting transfers between devices, local(): lax.all_to_all(sideband, 'tm', split_axis=0, concat_axis=0, tiled=True)  7.17 us
    all_to_all x1, starting transfers between devices, local(): lax.all_to_all(outgoing, 'tm', split_axis=0, concat_axis=0, tiled=True)  6.92 us
    dot_general x1, matrix products, window_sums(): jnp.einsum('ij,bjf->bif', lower, blocks, precision=lax.Precision.HIGHEST)  3.91 us
  transfers between devices with their start and end apart: 3, of which 1 were waited for; matrix products, arithmetic and copies ran while one was open for 36% of the time, Pallas kernels for 0%

profile of v1, /device:TPU:12, one launch (start us, length us, event | category | flops | bytes accessed | tf_op | source)
XLA Modules:
  0.0 127.0 jit_solution(14809261609317191149)
XLA Ops:
  0.0 1.0 reduce-window.14
  1.0 0.1 slice.54
  1.1 0.1 reduce-window.18
  1.1 0.1 slice_reduce_fusion.2
  1.2 1.4 %fusion.20 = (s32[]{:T(128)}, s32[4096]{0:T(1024)S(1)}) fusion(s32[4096]{0:T(1024)} %param.5, s32[32,128]{1,0:T(8,128)S(1)} %reduce-window.14, s32[32]{0:T(128)S(1)} %slice_reduce_fusion.2), kind=kLoop, calls=%fused_computation.53 | loop fusion | flops 32767 | bytes 49284 | tf_op jit(solution)/shard_map/reduce_sum | solution.py:61
  2.7 1.3 %fusion.7 = f32[4096,16]{1,0:T(8,128)S(1)} fusion(s32[4096]{0:T(1024)} %param.6), kind=kLoop, calls=%fused_computation.17 | loop fusion | flops 131072 | bytes 278528 | tf_op jit(solution)/shard_map/convert_element_type | solution.py:62
  4.0 20.2 %scatter_custom_fusion = f32[4096,144]{1,0:T(8,128)} fusion(s32[4096]{0:T(1024)S(1)} %get-tuple-element.10, f32[4096,16]{1,0:T(8,128)S(1)} %fusion.7, f32[]{:T(128)} %constant.74, f32[4096,128]{1,0:T(8,128)} %param.4, f32[]{:T(128)} %constant.14.clone.1), kind=kCustom, calls=%fused_computation.3 | custom fusion | flops 589824 | bytes 6553608 | tf_op jit(solution)/shard_map/scatter | solution.py:47
  24.2 1.7 %slice.58 = f32[4096,128]{1,0:T(8,128)S(1)} slice(f32[4096,144]{1,0:T(8,128)} %scatter_custom_fusion), slice={[0:4096], [0:128]} | slice | bytes 4194304 | tf_op jit(solution)/shard_map/slice | solution.py:65
  25.9 0.0 copy-start
  27.3 0.0 copy-done
  27.3 0.0 slice-start
  27.3 1.5 %collective-permute-start = (f32[512,128]{1,0:T(8,128)S(1)}, f32[512,128]{1,0:T(8,128)S(1)}, u32[]{:S(2)}, u32[]{:S(2)}) collective-permute-start(f32[512,128]{1,0:T(8,128)S(1)} %constant_dynamic-slice_fusion), channel_id=1, source_target_pairs={{0,2},{2,4},{4,6},{6,8},{8,10},{10,12},{12,14},{14,16},{16,18},{18... | collective-permute-start | bytes 786440 | tf_op jit(solution)/shard_map/ppermute | solution.py:14
  28.9 0.0 slice-done
  28.9 3.4 %convolution_bitcast_fusion.1 = f32[8,512,16]{1,2,0:T(8,128)S(1)} fusion(f32[8,512,16]{2,1,0:T(8,128)S(1)} %bitcast.54), kind=kOutput, calls=%fused_computation.19 | convolution fusion | flops 402915328 | bytes 524288 | tf_op jit(solution)/shard_map/ij,bjc->bic/dot_general | solution.py:33
  32.3 0.2 slice_reduce_fusion.1
  32.5 0.7 copy.33
  33.2 7.2 %all-to-all-start = ((f32[16,1,1]{2,1,0:T(1,128)}), f32[16,1,1]{2,1,0:T(1,128)S(1)}, u32[]{:S(2)}, u32[]{:S(2)}) async-start(f32[16,1,1]{2,1,0:T(1,128)} %copy.33), calls=%async_computation | async-start | bytes 16384 | tf_op jit(solution)/shard_map/all_to_all | solution.py:93
  40.4 0.2 fusion.22
  40.5 3.5 %fusion.15 = f32[1,4096]{1,0:T(1,128)S(1)} fusion(f32[4096,144]{1,0:T(8,128)} %scatter_custom_fusion), kind=kOutput, calls=%fused_computation.45 | convolution fusion | flops 786448 | bytes 2113536 | tf_op jit(solution)/shard_map/dot_general | solution.py:68
  44.0 0.1 broadcast_add_fusion
  44.1 0.6 copy.43
  44.8 0.0 copy-start.1
  44.8 2.6 %fusion.5 = f32[4096]{0:T(1024)S(1)} fusion(f32[8,512,16]{2,1,0:T(8,128)S(1)} %copy.43, f32[4096,144]{1,0:T(8,128)} %scatter_custom_fusion), kind=kLoop, calls=%fused_computation.13 | loop fusion | flops 126976 | bytes 540672 | tf_op jit(solution)/shard_map/reduce_sum | solution.py:37
  47.3 0.7 compare_select_fusion.1
  48.0 0.0 collective-permute-done
  48.0 0.0 copy-done.1
  48.0 0.2 pad_maximum_fusion
  48.2 3.9 %convolution_bitcast_fusion = f32[9,512,128]{1,2,0:T(8,128)S(1)} fusion(f32[9,512,128]{2,1,0:T(8,128)S(1)} %bitcast.55), kind=kOutput, calls=%fused_computation.18 | convolution fusion | flops 3624140800 | bytes 4718592 | tf_op jit(solution)/shard_map/ij,bjf->bif/dot_general | solution.py:21
  52.1 0.4 slice_reduce_fusion
  52.5 1.8 %multiply_reduce_fusion = (f32[8,512]{1,0:T(8,128)S(1)}, f32[8,512,128]{1,2,0:T(8,128)}) fusion(f32[9,512,128]{1,2,0:T(8,128)S(1)} %convolution_bitcast_fusion, f32[8,128]{1,0:T(8,128)S(1)} %slice_reduce_fusion), kind=kLoop, calls=%fused_computation.14 | loop fusion | flops 2093056 | bytes 6311936 | tf_op jit(solution)/shard_map/reduce_sum | solution.py:79
  54.2 0.0 copy-start.2
  54.2 1.9 %copy.38 = f32[8,512,128]{2,1,0:T(8,128)S(1)} copy(f32[8,512,128]{1,2,0:T(8,128)} %get-tuple-element.8) | data formatting | bytes 4194304 | tf_op jit(solution)/shard_map/sub | solution.py:23
  56.2 1.8 %all-gather = f32[2,1,4096]{2,1,0:T(1,128)S(1)} all-gather(f32[1,1,4096]{2,1,0:T(1,128)S(1)} %reshape.220), channel_id=1, replica_groups=mesh['tm'=16,'rep'=2] {'rep'}, dimensions={0}, use_global_device_ids=true | all-gather | bytes 49152 | tf_op jit(solution)/shard_map/all_gather | solution.py:82
  58.1 0.0 copy-done.2
  58.1 1.9 %fusion.4 = f32[4096,128]{1,0:T(8,128)} fusion(f32[8,512,128]{2,1,0:T(8,128)S(1)} %copy.38, f32[4096]{0:T(1024)S(1)} %add_sqrt_fusion, f32[128]{0:T(128)S(1)} %copy-done.2), kind=kLoop, calls=%fused_computation.11 | loop fusion | flops 1048576 | bytes 4211200 | tf_op jit(solution)/shard_map/div | solution.py:85
  60.0 12.1 %scatter_custom_fusion.1 = f32[3072,128]{1,0:T(8,128)} fusion(s32[4096]{0:T(1024)S(1)} %compare_select_fusion.1, f32[4096,128]{1,0:T(8,128)} %fusion.4, f32[]{:T(128)} %constant.14.clone.1), kind=kCustom, calls=%fused_computation.24 | custom fusion | bytes 1573376 | tf_op jit(solution)/shard_map/scatter | solution.py:52
  72.1 0.0 all-to-all-done
  72.1 6.9 %all-to-all-start.1 = ((f32[16,1,24576]{2,1,0:T(1,128)}), f32[16,1,24576]{2,1,0:T(1,128)S(1)}, u32[]{:S(2)}, u32[]{:S(2)}) async-start(f32[16,1,24576]{2,1,0:T(1,128)} %bitcast.29), calls=%async_computation.1 | async-start | bytes 3145728 | tf_op jit(solution)/shard_map/all_to_all | solution.py:92
  79.1 0.1 reduce.4
  79.2 0.4 convert_reduce_fusion.1
  79.6 0.7 fusion.21
  80.3 0.1 convert_reduce_fusion
  80.5 9.9 %compare_and_fusion = (pred[3072]{0:T(1024)(128)(4,1)S(1)}, s32[3072]{0:T(1024)S(1)}) fusion(s32[]{:T(128)} %bitcast.22, s32[]{:T(128)} %bitcast.21, s32[]{:T(128)} %bitcast.20, s32[]{:T(128)} %bitcast.19, s32[]{:T(128)} %bitcast.18, s32[]{:T(128)} %bitcast.17, s32[]{:T(128)} %bitcast.16, s32[]{:T(128)} %bitcast.15, s32[]{:T(128)} %bitcast.14, s32[]{:T(128)} %bitcast.13, ...), kind=kLoop, calls=%fused_computation.42 | loop fusion | flops 110592 | bytes 27712 | tf_op jit(solution)/shard_map/and | solution.py:103
  90.5 25.9 %all-to-all-done.1 = f32[16,1,24576]{2,1,0:T(1,128)S(1)} async-done(((f32[16,1,24576]{2,1,0:T(1,128)}), f32[16,1,24576]{2,1,0:T(1,128)S(1)}, u32[]{:S(2)}, u32[]{:S(2)}) %all-to-all-start.1) | async-done | bytes 1572896 | tf_op jit(solution)/shard_map/all_to_all | solution.py:92
  116.4 8.1 %gather_fusion = f32[3072,128]{1,0:T(8,128)S(1)} fusion(f32[3072,128]{1,0:T(8,128)S(1)} %bitcast.53, s32[3072]{0:T(1024)S(1)} %broadcast_clamp_fusion), kind=kCustom, calls=%fused_computation | custom fusion | bytes 3158016 | tf_op jit(solution)/shard_map/gather | solution.py:106
  124.5 2.5 %broadcast_select_fusion = f32[3072,128]{1,0:T(8,128)} fusion(f32[3072,128]{1,0:T(8,128)S(1)} %gather_fusion, pred[3072]{0:T(1024)(128)(4,1)S(1)} %get-tuple-element.5), kind=kLoop, calls=%fused_computation.23 | loop fusion | flops 393216 | bytes 3148800 | tf_op jit(solution)/shard_map/jit(_where)/select_n | solution.py:106
  (11 shorter events, 0.2 us)
Async XLA Ops:
  25.9 1.4 %copy-start = (f32[4096,128]{1,0:T(8,128)}, f32[4096,128]{1,0:T(8,128)S(1)}, u32[]{:S(2)}) copy-start(f32[4096,128]{1,0:T(8,128)S(1)} %slice.58) | copy-start | bytes 6291460
  27.3 1.6 %slice-start = ((f32[4096,144]{1,0:T(8,128)}), f32[4096,16]{1,0:T(8,128)S(1)}, s32[]{:S(2)}) async-start(f32[4096,144]{1,0:T(8,128)} %scatter_custom_fusion), calls=%async_computation.2 | async-start | bytes 4194304 | tf_op jit(solution)/shard_map/slice | solution.py:66
  27.3 20.7 %collective-permute-start = (f32[512,128]{1,0:T(8,128)S(1)}, f32[512,128]{1,0:T(8,128)S(1)}, u32[]{:S(2)}, u32[]{:S(2)}) collective-permute-start(f32[512,128]{1,0:T(8,128)S(1)} %constant_dynamic-slice_fusion), channel_id=1, source_target_pairs={{0,2},{2,4},{4,6},{6,8},{8,10},{10,12},{12,14},{14,16},{16,18},{18... | collective-permute-start | bytes 786440 | tf_op jit(solution)/shard_map/ppermute | solution.py:14
  33.2 38.9 %all-to-all-start = ((f32[16,1,1]{2,1,0:T(1,128)}), f32[16,1,1]{2,1,0:T(1,128)S(1)}, u32[]{:S(2)}, u32[]{:S(2)}) async-start(f32[16,1,1]{2,1,0:T(1,128)} %copy.33), calls=%async_computation | async-start | bytes 16384 | tf_op jit(solution)/shard_map/all_to_all | solution.py:93
  44.8 3.3 %copy-start.1 = (f32[4096,128]{1,0:T(8,128)S(1)}, f32[4096,128]{1,0:T(8,128)}, u32[]{:S(2)}) copy-start(f32[4096,128]{1,0:T(8,128)} %copy-done) | copy-start | bytes 6291460
  54.2 3.9 %copy-start.2 = (f32[128]{0:T(128)S(1)}, f32[128]{0:T(128)}, u32[]{:S(2)}) copy-start(f32[128]{0:T(128)} %param.7) | copy-start | bytes 1540
  72.1 44.2 %all-to-all-start.1 = ((f32[16,1,24576]{2,1,0:T(1,128)}), f32[16,1,24576]{2,1,0:T(1,128)S(1)}, u32[]{:S(2)}, u32[]{:S(2)}) async-start(f32[16,1,24576]{2,1,0:T(1,128)} %bitcast.29), calls=%async_computation.1 | async-start | bytes 3145728 | tf_op jit(solution)/shard_map/all_to_all | solution.py:92
